TPU v7x, 32 devices: a whole 2x2x4 slice. The times are simulated.
32 devices in a mesh: outer: 4 (over y, core), inner: 8 (over z, x).
Axes of the slice: x: 2, y: 2, z: 4, core: 2. Of those that a mesh axis runs over, the one named last changes fastest.
Arguments:
- queries: bfloat16 [4096, 4096], P(('outer', 'inner')), may hold values from -40 to 40
- keys: bfloat16 [4096, 512], P(('outer', 'inner')), may hold values from -4 to 4
- values: bfloat16 [4096, 512], P(('outer', 'inner')), may hold values from -6 to 6
- doc_lengths: int32 [16], replicated, may hold values from 1 to 1024, 4096 in all
Outputs:
- attended: bfloat16 [4096, 4096], P(('outer', 'inner'))
All inputs are finite; a program needn't handle non-finite values.
Results may differ from a plain program's by a relative error of at most 0.005.
Values may be sent and summed in bfloat16 or wider, within the bound.
No kernel may reach another device: no remote copies, remote signals or barrier semaphores. Data moves between devices by JAX's collectives and lax.ppermute only.
A program may use at most 256 MiB of HBM per device.

v0:
```python
import jax
import jax.numpy as jnp
from jax import lax
from jax.sharding import PartitionSpec as P

HEADS = 32
GROUPS = 4
HEAD_DIM = 128
OUTER_STEPS = 2


NEGATIVE = -1e30


def from_behind(array, axis, by):
    size = lax.axis_size(axis)
    pairs = [(i, i + by) for i in range(size) if 0 <= i + by < size]
    return lax.ppermute(array, axis, pairs)


def doc_of(positions, ends):
    return jnp.sum((positions[:, None] >= ends[None, :]).astype(jnp.int32), axis=1)


def tile_update(state, query4, key_rows, value_rows, allowed, scale):
    acc, top, total = state
    scores = (
        jnp.einsum("qghd,kgd->qghk", query4, key_rows, preferred_element_type=jnp.float32) * scale
    )
    scores = jnp.where(allowed[:, None, None, :], scores, NEGATIVE)
    new_top = jnp.maximum(top, jnp.max(scores, axis=3))
    weights = jnp.where(allowed[:, None, None, :], jnp.exp(scores - new_top[:, :, :, None]), 0.0)
    fade = jnp.exp(top - new_top)
    total = total * fade + jnp.sum(weights, axis=3)
    mixed = jnp.einsum(
        "qghk,kgd->qghd",
        weights.astype(jnp.bfloat16),
        value_rows,
        preferred_element_type=jnp.float32,
    )
    acc = acc * fade[:, :, :, None] + mixed
    return (acc, new_top, total)


def attend_tile(state, query4, qpos, qdoc, key_rows, value_rows, kpos, ends, scale):
    kdoc = doc_of(kpos, ends)
    allowed = (
        (kpos[None, :] <= qpos[:, None]) & (kpos[None, :] >= 0) & (kdoc[None, :] == qdoc[:, None])
    )
    return tile_update(state, query4, key_rows, value_rows, allowed, scale)


def attend_rows(state, query4, qpos, qdoc, key_rows, value_rows, kpos, ends, scale):
    count = key_rows.shape[0]
    width = 512
    key_tiles = key_rows.reshape(count // width, width, GROUPS, HEAD_DIM)
    value_tiles = value_rows.reshape(count // width, width, GROUPS, HEAD_DIM)
    pos_tiles = kpos.reshape(count // width, width)

    def visit(carry, item):
        return (
            attend_tile(carry, query4, qpos, qdoc, item[0], item[1], item[2], ends, scale),
            None,
        )

    state, unused = lax.scan(visit, state, (key_tiles, value_tiles, pos_tiles))
    return state


def body(queries, keys, values, doc_lengths):
    tokens = queries.shape[0]
    per_group = HEADS // GROUPS
    scale = HEAD_DIM ** (-0.5)
    n_inner = lax.axis_size("inner")
    outer_index = lax.axis_index("outer")
    inner_index = lax.axis_index("inner")
    block = tokens * n_inner
    ends = jnp.cumsum(doc_lengths)
    query4 = queries.reshape(tokens, GROUPS, per_group, HEAD_DIM)
    qpos = outer_index * block + inner_index * tokens + jnp.arange(tokens, dtype=jnp.int32)
    qdoc = doc_of(qpos, ends)
    fresh = (
        jnp.zeros((tokens, GROUPS, per_group, HEAD_DIM), jnp.float32),
        jnp.full((tokens, GROUPS, per_group), NEGATIVE, jnp.float32),
        jnp.zeros((tokens, GROUPS, per_group), jnp.float32),
    )
    key_list = [keys]
    value_list = [values]
    for step in range(1, OUTER_STEPS + 1):
        far_pair = from_behind((keys, values), "outer", step)
        key_list.append(far_pair[0])
        value_list.append(far_pair[1])
    stack_keys = jnp.concatenate(key_list, 0)
    stack_values = jnp.concatenate(value_list, 0)
    window = (OUTER_STEPS + 1) * tokens
    piece = (
        lax.all_gather(stack_keys, "inner", axis=0, tiled=True),
        lax.all_gather(stack_values, "inner", axis=0, tiled=True),
    )
    rows = jnp.arange(piece[0].shape[0], dtype=jnp.int32)
    owner = rows // window
    within = rows % window
    kpos = (outer_index - within // tokens) * block + owner * tokens + within % tokens
    state = attend_rows(fresh, query4, qpos, qdoc, piece[0], piece[1], kpos, ends, scale)
    result = state[0] / state[2][:, :, :, None]
    return result.astype(jnp.bfloat16).reshape(tokens, HEADS * HEAD_DIM)


def solution(mesh):
    in_specs = (
        P(("outer", "inner"), None),
        P(("outer", "inner"), None),
        P(("outer", "inner"), None),
        P(),
    )
    out_specs = P(("outer", "inner"), None)
    return jax.shard_map(body, mesh=mesh, in_specs=in_specs, out_specs=out_specs, check_vma=False)
```

profile of v0, /device:TPU:0, one launch (start us, length us, event | category | flops | bytes accessed | tf_op | source)
XLA Modules:
  0.0 214.8 jit_solution(8807723948208973916)
XLA Ops:
  6.5 2.4 %collective-permute-start = (bf16[128,512]{1,0:T(8,128)(2,1)}, bf16[128,512]{1,0:T(8,128)(2,1)S(1)}, u32[]{:S(2)}, u32[]{:S(2)}) collective-permute-start(bf16[128,512]{1,0:T(8,128)(2,1)} %param.7), channel_id=1, source_target_pairs={{0,8},{8,16},{16,24},{1,9},{9,17},{17,25},{2,10},{10,18},{18,26},{... | collective-permute-start | bytes 393224 | tf_op jit(solution)/shard_map/ppermute | solution.py:18
  8.9 4.4 %collective-permute-start.1 = (bf16[128,512]{1,0:T(8,128)(2,1)}, bf16[128,512]{1,0:T(8,128)(2,1)S(1)}, u32[]{:S(2)}, u32[]{:S(2)}) collective-permute-start(bf16[128,512]{1,0:T(8,128)(2,1)} %param.7), channel_id=1, source_target_pairs={{0,16},{8,24},{1,17},{9,25},{2,18},{10,26},{3,19},{11,27},{4,20},{... | collective-permute-start | bytes 393224 | tf_op jit(solution)/shard_map/ppermute | solution.py:18
  13.4 3.1 %collective-permute-done.1 = bf16[128,512]{1,0:T(8,128)(2,1)S(1)} collective-permute-done((bf16[128,512]{1,0:T(8,128)(2,1)}, bf16[128,512]{1,0:T(8,128)(2,1)S(1)}, u32[]{:S(2)}, u32[]{:S(2)}) %collective-permute-start.1) | collective-permute-done | bytes 131104 | tf_op jit(solution)/shard_map/ppermute | solution.py:18
  16.5 1.7 pad_maximum_fusion
  18.2 1.3 collective-permute-start.2
  19.5 4.9 %collective-permute-start.3 = (bf16[128,512]{1,0:T(8,128)(2,1)}, bf16[128,512]{1,0:T(8,128)(2,1)S(1)}, u32[]{:S(2)}, u32[]{:S(2)}) collective-permute-start(bf16[128,512]{1,0:T(8,128)(2,1)} %param.8), channel_id=1, source_target_pairs={{0,16},{8,24},{1,17},{9,25},{2,18},{10,26},{3,19},{11,27},{4,20},{... | collective-permute-start | bytes 393224 | tf_op jit(solution)/shard_map/ppermute | solution.py:18
  24.4 3.1 %collective-permute-done.3 = bf16[128,512]{1,0:T(8,128)(2,1)S(1)} collective-permute-done((bf16[128,512]{1,0:T(8,128)(2,1)}, bf16[128,512]{1,0:T(8,128)(2,1)S(1)}, u32[]{:S(2)}, u32[]{:S(2)}) %collective-permute-start.3) | collective-permute-done | bytes 131104 | tf_op jit(solution)/shard_map/ppermute | solution.py:18
  27.5 1.7 pad_maximum_fusion.1
  29.3 0.7 copy.16
  30.2 1.6 copy.17
  31.8 0.7 copy.19
  32.6 47.8 %all-gather.3.cloned.1.call-done = bf16[3072,512]{1,0:T(8,128)(2,1)} async-done(((bf16[384,512]{1,0:T(8,128)(2,1)}), bf16[3072,512]{1,0:T(8,128)(2,1)}) %all-gather.3.cloned.1.call-update) | async-done | bytes 3145744 | tf_op jit(solution)/shard_map/all_gather | solution.py:97
  80.4 5.5 %reshape.113 = bf16[6,512,4,128]{3,2,1,0:T(4,128)(2,1)} reshape(bf16[3072,512]{1,0:T(8,128)(2,1)} %all-gather.3.cloned.1.call-done) | data formatting | bytes 6291456 | tf_op jit(solution)/shard_map/reshape | solution.py:56
  86.0 55.4 %all-gather.5.cloned.1.call-done = bf16[3072,512]{1,0:T(8,128)(2,1)} async-done(((bf16[384,512]{1,0:T(8,128)(2,1)}), bf16[3072,512]{1,0:T(8,128)(2,1)}) %all-gather.5.cloned.1.call-update) | async-done | bytes 3145744 | tf_op jit(solution)/shard_map/all_gather | solution.py:98
  141.3 5.5 %reshape.115 = bf16[6,512,4,128]{3,2,1,0:T(4,128)(2,1)} reshape(bf16[3072,512]{1,0:T(8,128)(2,1)} %all-gather.5.cloned.1.call-done) | data formatting | bytes 6291456 | tf_op jit(solution)/shard_map/reshape | solution.py:57
  146.8 57.9 %while.15 = (s32[]{:T(128)}, f32[128,4,8,128]{0,3,2,1:T(8,128)}, f32[128,4,8]{0,2,1:T(8,128)S(1)}, f32[128,4,8]{0,2,1:T(8,128)S(1)}, s32[6,512]{1,0:T(8,128)S(1)...) while((s32[]{:T(128)}, f32[128,4,8,128]{0,3,2,1:T(8,128)}, ...), condition=%wide.region_6.7_spmd.clone, body=%wide.region_2.6_spmd.clone.sunk | while | flops 1102884992 | bytes 51919632 | solution.py:66
  147.2 1.6 constant_dynamic-slice_fusion.5
  149.1 1.4 fusion.41
  150.5 2.1 fusion.42
  152.6 2.5 %bitcast_add_fusion.2 = f32[128,4,8,128]{0,3,2,1:T(8,128)S(1)} fusion(f32[128,4,8,128]{0,3,2,1:T(8,128)S(1)} %copy-done, f32[4,512,128,8]{2,1,3,0:T(8,128)S(1)} %get-tuple-element.234, f32[128,4,8]{0,2,1:T(8,128)S(1)} %select_maximum_fusion.2, pred[128,512]{0,1:T(8,128)(4,1)S(1)} %compare_and_fusion.2, f32[128,4,8]{0,2,1:T(8,128)S(1)} %get-tuple-element.236, ...), kind=kOutput, calls=%fused_computation.8.clone.1 | convolution fusion | flops 548929536 | bytes 13205505 | tf_op jit(solution)/shard_map/while/body/eval_jaxpr/qghk,kgd->qghd/dot_general | solution.py:35
  155.2 1.3 copy-done.1
  156.9 1.6 constant_dynamic-slice_fusion.5
  158.8 1.4 fusion.41
  160.2 2.1 fusion.42
  162.3 2.5 %bitcast_add_fusion.2 = f32[128,4,8,128]{0,3,2,1:T(8,128)S(1)} fusion(f32[128,4,8,128]{0,3,2,1:T(8,128)S(1)} %copy-done, f32[4,512,128,8]{2,1,3,0:T(8,128)S(1)} %get-tuple-element.234, f32[128,4,8]{0,2,1:T(8,128)S(1)} %select_maximum_fusion.2, pred[128,512]{0,1:T(8,128)(4,1)S(1)} %compare_and_fusion.2, f32[128,4,8]{0,2,1:T(8,128)S(1)} %get-tuple-element.236, ...), kind=kOutput, calls=%fused_computation.8.clone.1 | convolution fusion | flops 548929536 | bytes 13205505 | tf_op jit(solution)/shard_map/while/body/eval_jaxpr/qghk,kgd->qghd/dot_general | solution.py:35
  164.8 1.3 copy-done.1
  166.5 1.6 constant_dynamic-slice_fusion.5
  168.4 1.4 fusion.41
  169.8 2.1 fusion.42
  171.9 2.5 %bitcast_add_fusion.2 = f32[128,4,8,128]{0,3,2,1:T(8,128)S(1)} fusion(f32[128,4,8,128]{0,3,2,1:T(8,128)S(1)} %copy-done, f32[4,512,128,8]{2,1,3,0:T(8,128)S(1)} %get-tuple-element.234, f32[128,4,8]{0,2,1:T(8,128)S(1)} %select_maximum_fusion.2, pred[128,512]{0,1:T(8,128)(4,1)S(1)} %compare_and_fusion.2, f32[128,4,8]{0,2,1:T(8,128)S(1)} %get-tuple-element.236, ...), kind=kOutput, calls=%fused_computation.8.clone.1 | convolution fusion | flops 548929536 | bytes 13205505 | tf_op jit(solution)/shard_map/while/body/eval_jaxpr/qghk,kgd->qghd/dot_general | solution.py:35
  174.5 1.3 copy-done.1
  176.2 1.6 constant_dynamic-slice_fusion.5
  178.1 1.4 fusion.41
  179.5 2.1 fusion.42
  181.6 2.5 %bitcast_add_fusion.2 = f32[128,4,8,128]{0,3,2,1:T(8,128)S(1)} fusion(f32[128,4,8,128]{0,3,2,1:T(8,128)S(1)} %copy-done, f32[4,512,128,8]{2,1,3,0:T(8,128)S(1)} %get-tuple-element.234, f32[128,4,8]{0,2,1:T(8,128)S(1)} %select_maximum_fusion.2, pred[128,512]{0,1:T(8,128)(4,1)S(1)} %compare_and_fusion.2, f32[128,4,8]{0,2,1:T(8,128)S(1)} %get-tuple-element.236, ...), kind=kOutput, calls=%fused_computation.8.clone.1 | convolution fusion | flops 548929536 | bytes 13205505 | tf_op jit(solution)/shard_map/while/body/eval_jaxpr/qghk,kgd->qghd/dot_general | solution.py:35
  184.2 1.3 copy-done.1
  185.8 1.6 constant_dynamic-slice_fusion.5
  187.8 1.4 fusion.41
  189.1 2.1 fusion.42
  191.3 2.5 %bitcast_add_fusion.2 = f32[128,4,8,128]{0,3,2,1:T(8,128)S(1)} fusion(f32[128,4,8,128]{0,3,2,1:T(8,128)S(1)} %copy-done, f32[4,512,128,8]{2,1,3,0:T(8,128)S(1)} %get-tuple-element.234, f32[128,4,8]{0,2,1:T(8,128)S(1)} %select_maximum_fusion.2, pred[128,512]{0,1:T(8,128)(4,1)S(1)} %compare_and_fusion.2, f32[128,4,8]{0,2,1:T(8,128)S(1)} %get-tuple-element.236, ...), kind=kOutput, calls=%fused_computation.8.clone.1 | convolution fusion | flops 548929536 | bytes 13205505 | tf_op jit(solution)/shard_map/while/body/eval_jaxpr/qghk,kgd->qghd/dot_general | solution.py:35
  193.8 1.3 copy-done.1
  195.5 1.6 constant_dynamic-slice_fusion.5
  197.4 1.4 fusion.41
  198.8 2.1 fusion.42
  200.9 2.5 %bitcast_add_fusion.2 = f32[128,4,8,128]{0,3,2,1:T(8,128)S(1)} fusion(f32[128,4,8,128]{0,3,2,1:T(8,128)S(1)} %copy-done, f32[4,512,128,8]{2,1,3,0:T(8,128)S(1)} %get-tuple-element.234, f32[128,4,8]{0,2,1:T(8,128)S(1)} %select_maximum_fusion.2, pred[128,512]{0,1:T(8,128)(4,1)S(1)} %compare_and_fusion.2, f32[128,4,8]{0,2,1:T(8,128)S(1)} %get-tuple-element.236, ...), kind=kOutput, calls=%fused_computation.8.clone.1 | convolution fusion | flops 548929536 | bytes 13205505 | tf_op jit(solution)/shard_map/while/body/eval_jaxpr/qghk,kgd->qghd/dot_general | solution.py:35
  203.5 1.3 copy-done.1
  204.8 1.8 divide_convert_fusion
  206.6 1.3 copy.25
  (80 shorter events, 4.8 us)
Async XLA Ops:
  6.5 73.9 %all-gather.3.cloned.1.call-start = ((), (), s32[]{:S(2)}) async-start(), calls=%async_computation | async-start | bytes 3538944 | tf_op jit(solution)/shard_map/all_gather | solution.py:97
  6.5 6.8 %collective-permute-start = (bf16[128,512]{1,0:T(8,128)(2,1)}, bf16[128,512]{1,0:T(8,128)(2,1)S(1)}, u32[]{:S(2)}, u32[]{:S(2)}) collective-permute-start(bf16[128,512]{1,0:T(8,128)(2,1)} %param.7), channel_id=1, source_target_pairs={{0,8},{8,16},{16,24},{1,9},{9,17},{17,25},{2,10},{10,18},{18,26},{... | collective-permute-start | bytes 393224 | tf_op jit(solution)/shard_map/ppermute | solution.py:18
  8.9 7.5 %collective-permute-start.1 = (bf16[128,512]{1,0:T(8,128)(2,1)}, bf16[128,512]{1,0:T(8,128)(2,1)S(1)}, u32[]{:S(2)}, u32[]{:S(2)}) collective-permute-start(bf16[128,512]{1,0:T(8,128)(2,1)} %param.7), channel_id=1, source_target_pairs={{0,16},{8,24},{1,17},{9,25},{2,18},{10,26},{3,19},{11,27},{4,20},{... | collective-permute-start | bytes 393224 | tf_op jit(solution)/shard_map/ppermute | solution.py:18
  18.1 123.2 %all-gather.5.cloned.1.call-start = ((), (), s32[]{:S(2)}) async-start(), calls=%async_computation.1 | async-start | bytes 3538944 | tf_op jit(solution)/shard_map/all_gather | solution.py:98
  18.2 6.2 %collective-permute-start.2 = (bf16[128,512]{1,0:T(8,128)(2,1)}, bf16[128,512]{1,0:T(8,128)(2,1)S(1)}, u32[]{:S(2)}, u32[]{:S(2)}) collective-permute-start(bf16[128,512]{1,0:T(8,128)(2,1)} %param.8), channel_id=1, source_target_pairs={{0,8},{8,16},{16,24},{1,9},{9,17},{17,25},{2,10},{10,18},{18,26},{... | collective-permute-start | bytes 393224 | tf_op jit(solution)/shard_map/ppermute | solution.py:18
  19.5 8.0 %collective-permute-start.3 = (bf16[128,512]{1,0:T(8,128)(2,1)}, bf16[128,512]{1,0:T(8,128)(2,1)S(1)}, u32[]{:S(2)}, u32[]{:S(2)}) collective-permute-start(bf16[128,512]{1,0:T(8,128)(2,1)} %param.8), channel_id=1, source_target_pairs={{0,16},{8,24},{1,17},{9,25},{2,18},{10,26},{3,19},{11,27},{4,20},{... | collective-permute-start | bytes 393224 | tf_op jit(solution)/shard_map/ppermute | solution.py:18
  149.1 3.5 %copy-start = (f32[128,4,8,128]{0,3,2,1:T(8,128)S(1)}, f32[128,4,8,128]{0,3,2,1:T(8,128)}, u32[]{:S(2)}) copy-start(f32[128,4,8,128]{0,3,2,1:T(8,128)} %get-tuple-element.253) | copy-start | bytes 6291460 | tf_op jit(solution)/shard_map/while
  155.2 1.3 copy-start.1
  158.8 3.5 %copy-start = (f32[128,4,8,128]{0,3,2,1:T(8,128)S(1)}, f32[128,4,8,128]{0,3,2,1:T(8,128)}, u32[]{:S(2)}) copy-start(f32[128,4,8,128]{0,3,2,1:T(8,128)} %get-tuple-element.253) | copy-start | bytes 6291460 | tf_op jit(solution)/shard_map/while
  164.8 1.3 copy-start.1
  168.4 3.5 %copy-start = (f32[128,4,8,128]{0,3,2,1:T(8,128)S(1)}, f32[128,4,8,128]{0,3,2,1:T(8,128)}, u32[]{:S(2)}) copy-start(f32[128,4,8,128]{0,3,2,1:T(8,128)} %get-tuple-element.253) | copy-start | bytes 6291460 | tf_op jit(solution)/shard_map/while
  174.5 1.3 copy-start.1
  178.1 3.5 %copy-start = (f32[128,4,8,128]{0,3,2,1:T(8,128)S(1)}, f32[128,4,8,128]{0,3,2,1:T(8,128)}, u32[]{:S(2)}) copy-start(f32[128,4,8,128]{0,3,2,1:T(8,128)} %get-tuple-element.253) | copy-start | bytes 6291460 | tf_op jit(solution)/shard_map/while
  184.1 1.3 copy-start.1
  187.7 3.5 %copy-start = (f32[128,4,8,128]{0,3,2,1:T(8,128)S(1)}, f32[128,4,8,128]{0,3,2,1:T(8,128)}, u32[]{:S(2)}) copy-start(f32[128,4,8,128]{0,3,2,1:T(8,128)} %get-tuple-element.253) | copy-start | bytes 6291460 | tf_op jit(solution)/shard_map/while
  193.8 1.3 copy-start.1
  197.4 3.5 %copy-start = (f32[128,4,8,128]{0,3,2,1:T(8,128)S(1)}, f32[128,4,8,128]{0,3,2,1:T(8,128)}, u32[]{:S(2)}) copy-start(f32[128,4,8,128]{0,3,2,1:T(8,128)} %get-tuple-element.253) | copy-start | bytes 6291460 | tf_op jit(solution)/shard_map/while
  203.5 1.3 copy-start.1
Sparse Core Ops, SparseCore 0:
  18.3 62.1 all-gather.2
  82.6 58.6 all-gather.4
where the time goes:
time: 215 us
  waiting for transfers between devices  109 us (51%)
  local copies, waits for them, and re-layouts  34.5 us (16%)
  matrix products  23.4 us (11%)
  other arithmetic  20.4 us (9%)
  between operations  13.5 us (6%)
  starting transfers between devices  13.1 us (6%)
    all_gather x1, waiting for transfers between devices, body(): lax.all_gather(stack_values, 'inner', axis=0, tiled=True)  55.4 us
    all_gather x1, waiting for transfers between devices, body(): lax.all_gather(stack_keys, 'inner', axis=0, tiled=True)  47.8 us
    dot_general x6, matrix products, tile_update(): jnp.einsum('qghk,kgd->qghd', weights.astype(jnp.bfloat16), value_rows, pr...  15.2 us
    ppermute x4, starting transfers between devices, from_behind(): return lax.ppermute(array, axis, pairs)  13 us
    reduce_sum x6, other arithmetic, tile_update(): total = total * fade + jnp.sum(weights, axis=3)  12.4 us
    dynamic_slice x12, local copies, waits for them, and re-layouts, attend_rows(): state, unused = lax.scan(visit, state, (key_tiles, value_tiles, pos_tiles))  11.3 us
    dot_general x6, matrix products, tile_update(): jnp.einsum('qghd,kgd->qghk', query4, key_rows, preferred_element_type=jnp...  8.2 us
    while x30, local copies, waits for them, and re-layouts  7.81 us
  transfers between devices with their start and end apart: 6, of which 4 were waited for; matrix products, arithmetic and copies ran while one was open for 5% of the time, Pallas kernels for 0%

commit v1 on v0

--- a/solution.py
+++ b/solution.py
@@ -1,15 +1,26 @@
+import functools
+
 import jax
 import jax.numpy as jnp
 from jax import lax
+from jax.experimental import pallas as pl
+from jax.experimental.pallas import tpu as pltpu
 from jax.sharding import PartitionSpec as P
 
 HEADS = 32
 GROUPS = 4
 HEAD_DIM = 128
 OUTER_STEPS = 2
-
+PER_GROUP = HEADS // GROUPS
+LOG2E = 1.4426950408889634
 
 NEGATIVE = -1e30
+
+AXES = ("outer", "inner")
+
+
+def longest_document(seq):
+    return seq // 4
 
 
 def from_behind(array, axis, by):
@@ -63,26 +74,25 @@
             None,
         )
 
-    state, unused = lax.scan(visit, state, (key_tiles, value_tiles, pos_tiles))
+    state, _ = lax.scan(visit, state, (key_tiles, value_tiles, pos_tiles))
     return state
 
 
-def body(queries, keys, values, doc_lengths):
+def gathered_body(queries, keys, values, doc_lengths):
     tokens = queries.shape[0]
-    per_group = HEADS // GROUPS
     scale = HEAD_DIM ** (-0.5)
     n_inner = lax.axis_size("inner")
     outer_index = lax.axis_index("outer")
     inner_index = lax.axis_index("inner")
     block = tokens * n_inner
     ends = jnp.cumsum(doc_lengths)
-    query4 = queries.reshape(tokens, GROUPS, per_group, HEAD_DIM)
+    query4 = queries.reshape(tokens, GROUPS, PER_GROUP, HEAD_DIM)
     qpos = outer_index * block + inner_index * tokens + jnp.arange(tokens, dtype=jnp.int32)
     qdoc = doc_of(qpos, ends)
     fresh = (
-        jnp.zeros((tokens, GROUPS, per_group, HEAD_DIM), jnp.float32),
-        jnp.full((tokens, GROUPS, per_group), NEGATIVE, jnp.float32),
-        jnp.zeros((tokens, GROUPS, per_group), jnp.float32),
+        jnp.zeros((tokens, GROUPS, PER_GROUP, HEAD_DIM), jnp.float32),
+        jnp.full((tokens, GROUPS, PER_GROUP), NEGATIVE, jnp.float32),
+        jnp.zeros((tokens, GROUPS, PER_GROUP), jnp.float32),
     )
     key_list = [keys]
     value_list = [values]
@@ -106,12 +116,198 @@
     return result.astype(jnp.bfloat16).reshape(tokens, HEADS * HEAD_DIM)
 
 
+def attend_kernel(tokens, n_inner, slots, first, last, *refs):
+    refs = list(refs)
+    docs_ref = refs.pop(0) if first else None
+    q_ref = refs.pop(0)
+    kv_refs = [(refs.pop(0), refs.pop(0)) for _ in slots]
+    if not first:
+        acc_in, ml_in, rel_in = refs.pop(0), refs.pop(0), refs.pop(0)
+    if last:
+        out_ref = refs.pop(0)
+    else:
+        acc_out, ml_out = refs.pop(0), refs.pop(0)
+        if first:
+            rel_out = refs.pop(0)
+    lane = lax.broadcasted_iota(jnp.int32, (tokens, HEAD_DIM), 1)
+    if first:
+        base = (lax.axis_index("outer") * n_inner + lax.axis_index("inner")) * tokens
+        row = lax.broadcasted_iota(jnp.int32, (tokens, HEAD_DIM), 0)
+        rel = jnp.full((tokens, HEAD_DIM), -base, jnp.int32)
+        end = -base
+        for i in range(docs_ref.shape[0]):
+            end = end + docs_ref[i]
+            rel = jnp.where(row >= end, end, rel)
+        rel_out[...] = rel
+    else:
+        rel = rel_in[...]
+    odd = lax.rem(lax.axis_index("inner"), 2)
+    bias = []
+    for distance, sway in slots:
+        start = -tokens * (distance + sway * odd)
+        seen = lane + start >= rel
+        if distance == 0 and sway == 0:
+            seen = seen & (lane <= row)
+        bias.append(jnp.where(seen, 0.0, NEGATIVE).astype(jnp.float32))
+    bias = jnp.concatenate(bias, axis=1)
+    key_rows = jnp.concatenate([k[...] for k, _ in kv_refs], axis=0)
+    value_rows = jnp.concatenate([v[...] for _, v in kv_refs], axis=0)
+    factor = HEAD_DIM ** (-0.5) * LOG2E
+    ml = jnp.zeros((tokens, HEAD_DIM), jnp.float32)
+    for h in range(PER_GROUP):
+        cols = slice(h * HEAD_DIM, (h + 1) * HEAD_DIM)
+        scores = lax.dot_general(
+            q_ref[:, cols], key_rows, (((1,), (1,)), ((), ())), preferred_element_type=jnp.float32
+        )
+        scores = scores + bias
+        top = jnp.max(scores, axis=1, keepdims=True)
+        if not first:
+            old_top = ml_in[0, :, h : h + 1]
+            top = jnp.maximum(top, old_top)
+            fade = jnp.exp2((old_top - top) * factor)
+        weights = jnp.exp2((scores - top) * factor)
+        total = jnp.sum(weights, axis=1, keepdims=True)
+        mixed = lax.dot_general(
+            weights.astype(jnp.bfloat16),
+            value_rows,
+            (((1,), (0,)), ((), ())),
+            preferred_element_type=jnp.float32,
+        )
+        if not first:
+            total = total + ml_in[0, :, PER_GROUP + h : PER_GROUP + h + 1] * fade
+            mixed = mixed + acc_in[:, cols] * fade
+        if last:
+            out_ref[:, cols] = (mixed / total).astype(out_ref.dtype)
+        else:
+            acc_out[:, cols] = mixed
+            ml = jnp.where(lane == h, top, ml)
+            ml = jnp.where(lane == PER_GROUP + h, total, ml)
+    if not last:
+        ml_out[0] = ml
+
+
+def attend(queries, docs, slots, state, last, n_inner):
+    tokens = queries.shape[0]
+    first = state is None
+    wide = PER_GROUP * HEAD_DIM
+    wide_spec = pl.BlockSpec((tokens, wide), lambda g: (0, g))
+    ml_spec = pl.BlockSpec((1, tokens, HEAD_DIM), lambda g: (g, 0, 0))
+    rel_spec = pl.BlockSpec((tokens, HEAD_DIM), lambda g: (0, 0))
+    args, specs = [], []
+    if first:
+        args.append(docs)
+        specs.append(pl.BlockSpec(memory_space=pltpu.SMEM))
+    args.append(queries)
+    specs.append(wide_spec)
+    for (k, v), _, _ in slots:
+        if k is v:
+            args += [k, k]
+            specs.append(pl.BlockSpec((tokens, HEAD_DIM), lambda g: (0, g)))
+            specs.append(pl.BlockSpec((tokens, HEAD_DIM), lambda g: (0, g + GROUPS)))
+        else:
+            args += [k, v]
+            specs += [pl.BlockSpec((tokens, HEAD_DIM), lambda g: (0, g))] * 2
+    if not first:
+        args += list(state)
+        specs += [wide_spec, ml_spec, rel_spec]
+    if last:
+        out_shape = jax.ShapeDtypeStruct((tokens, HEADS * HEAD_DIM), jnp.bfloat16)
+        out_specs = wide_spec
+    else:
+        out_shape = [
+            jax.ShapeDtypeStruct((tokens, HEADS * HEAD_DIM), jnp.float32),
+            jax.ShapeDtypeStruct((GROUPS, tokens, HEAD_DIM), jnp.float32),
+        ]
+        out_specs = [wide_spec, ml_spec]
+        if first:
+            out_shape.append(jax.ShapeDtypeStruct((tokens, HEAD_DIM), jnp.int32))
+            out_specs.append(rel_spec)
+    keys_seen = len(slots) * tokens
+    result = pl.pallas_call(
+        functools.partial(
+            attend_kernel, tokens, n_inner, tuple((d, s) for _, d, s in slots), first, last
+        ),
+        grid=(GROUPS,),
+        in_specs=specs,
+        out_specs=out_specs,
+        out_shape=out_shape,
+        cost_estimate=pl.CostEstimate(
+            flops=4 * HEADS * HEAD_DIM * tokens * keys_seen,
+            bytes_accessed=tokens * HEADS * HEAD_DIM * 8,
+            transcendentals=HEADS * tokens * keys_seen,
+        ),
+        compiler_params=pltpu.CompilerParams(
+            dimension_semantics=("arbitrary",), vmem_limit_bytes=24 * 1024 * 1024
+        ),
+    )(*args)
+    if last:
+        return result
+    return (result[0], result[1], state[2] if not first else result[2])
+
+
+def window_body(reach, queries, keys, values, doc_lengths):
+    n_inner = lax.axis_size("inner")
+    shards = lax.axis_size("outer") * n_inner
+    half = reach // 2
+
+    def move(array, pairs):
+        return lax.ppermute(array, AXES, pairs)
+
+    def behind(array, by):
+        return move(array, [(s, s + 2 * by) for s in range(shards - 2 * by)])
+
+    swap = [(s, s ^ 1) for s in range(shards)]
+    own = jnp.concatenate([keys, values], axis=1)
+    near = {1: behind(own, 1)}
+    side = {0: move(own, swap)}
+    for k in range(3, half):
+        near[k] = behind(own, k)
+    near[half] = behind(own, half)
+    side[1] = move(near[1], swap)
+    if half > 2:
+        near[2] = behind(near[1], 1)
+    for k in range(3, half):
+        side[k] = move(near[k], swap)
+    far = move(side[0], [(s, s + 2 * half) for s in range(shards - 2 * half) if s % 2 == 0])
+    if half > 2:
+        side[2] = move(near[2], swap)
+    odd = lax.axis_index("inner") % 2 == 1
+    edge = jnp.where(odd, side[0], far)
+
+    def slot_near(k):
+        return ((near[k], near[k]), 2 * k, 0)
+
+    def slot_side(k):
+        return ((side[k], side[k]), 2 * k - 1, 2)
+
+    early = [((keys, values), 0, 0), slot_near(1)]
+    middle = [((edge, edge), 2 * half - 1, 2 - 2 * half)]
+    middle += [slot_side(1)]
+    for k in range(3, half):
+        middle += [slot_near(k), slot_side(k)]
+    middle += [slot_near(half)]
+    if half > 2:
+        middle += [slot_near(2)]
+    state = attend(queries, doc_lengths, early, None, False, n_inner)
+    if half > 2:
+        state = attend(queries, None, middle, state, False, n_inner)
+        return attend(queries, None, [slot_side(2)], state, True, n_inner)
+    return attend(queries, None, middle, state, True, n_inner)
+
+
 def solution(mesh):
-    in_specs = (
-        P(("outer", "inner"), None),
-        P(("outer", "inner"), None),
-        P(("outer", "inner"), None),
-        P(),
-    )
-    out_specs = P(("outer", "inner"), None)
-    return jax.shard_map(body, mesh=mesh, in_specs=in_specs, out_specs=out_specs, check_vma=False)
+    in_specs = (P(AXES, None), P(AXES, None), P(AXES, None), P())
+    out_specs = P(AXES, None)
+    shards = mesh.shape["outer"] * mesh.shape["inner"]
+
+    def run(queries, keys, values, doc_lengths):
+        seq = queries.shape[0]
+        tokens = seq // shards
+        reach = -(-(longest_document(seq) - 1) // tokens)
+        short = reach <= mesh.shape["inner"] and reach % 2 == 0 and mesh.shape["inner"] % 2 == 0
+        body = functools.partial(window_body, reach) if short else gathered_body
+        return jax.shard_map(
+            body, mesh=mesh, in_specs=in_specs, out_specs=out_specs, check_vma=False
+        )(queries, keys, values, doc_lengths)
+
+    return run

time: 215 us -> 68.1 us (0.32)
  the two profiles are of different devices: /device:TPU:0 before, /device:TPU:16 now
where the time goes in v1:
time: 68.1 us; the launch traced here: 67.8 us
  Pallas kernels  31.5 us (46%)
  starting transfers between devices  22.5 us (33%)
  waiting for transfers between devices  8.17 us (12%)
  local copies, waits for them, and re-layouts  5.52 us (8%)
    pallas_call x3, Pallas kernels, attend(): pl.pallas_call(functools.partial(attend_kernel, tokens, n_inner, tuple(((...  31.5 us
    ppermute x9, starting transfers between devices, move(): return lax.ppermute(array, AXES, pairs)  22.5 us
    ppermute x9, waiting for transfers between devices, move(): return lax.ppermute(array, AXES, pairs)  8.17 us
    unnamed x11, local copies, waits for them, and re-layouts  4.6 us
  transfers between devices with their start and end apart: 9, of which 2 were waited for; matrix products, arithmetic and copies ran while one was open for 0% of the time, Pallas kernels for 29%

profile of v1, /device:TPU:16, one launch (start us, length us, event | category | flops | bytes accessed | tf_op | source)
XLA Modules:
  0.0 67.8 jit_solution(4074372420067844976)
XLA Ops:
  0.0 0.9 %constant_dynamic-update-slice_fusion.1 = bf16[128,1024]{1,0:T(8,128)(2,1)S(1)} fusion(bf16[128,512]{1,0:T(8,128)(2,1)} %refs_2_.1), kind=kLoop, calls=%fused_computation.2 | loop fusion | bytes 262144
  0.9 0.9 %constant_dynamic-update-slice_fusion = bf16[128,1024]{1,0:T(8,128)(2,1)S(1)} fusion(bf16[128,1024]{1,0:T(8,128)(2,1)S(1)} %constant_dynamic-update-slice_fusion.1, bf16[128,512]{1,0:T(8,128)(2,1)} %refs_3_.1), kind=kLoop, calls=%fused_computation.1 | loop fusion | bytes 262144 | tf_op jit(solution)/shard_map/concatenate | solution.py:260
  1.8 3.5 %collective-permute-start = (bf16[128,1024]{1,0:T(8,128)(2,1)S(1)}, bf16[128,1024]{1,0:T(8,128)(2,1)S(1)}, u32[]{:S(2)}, u32[]{:S(2)}) collective-permute-start(bf16[128,1024]{1,0:T(8,128)(2,1)S(1)} %constant_dynamic-update-slice_fusion), channel_id=1, source_target_pairs={{0,2},{1,3},{2,4},{3,5},{4,6},{5,7},{6,8},{7,9},{8,10},{9,11},{10,... | collective-permute-start | bytes 786440 | tf_op jit(solution)/shard_map/ppermute | solution.py:254
  5.3 1.6 %collective-permute-start.3 = (bf16[128,1024]{1,0:T(8,128)(2,1)S(1)}, bf16[128,1024]{1,0:T(8,128)(2,1)S(1)}, u32[]{:S(2)}, u32[]{:S(2)}) collective-permute-start(bf16[128,1024]{1,0:T(8,128)(2,1)S(1)} %constant_dynamic-update-slice_fusion), channel_id=1, source_target_pairs={{0,1},{1,0},{2,3},{3,2},{4,5},{5,4},{6,7},{7,6},{8,9},{9,8},{10,11... | collective-permute-start | bytes 786440 | tf_op jit(solution)/shard_map/ppermute | solution.py:254
  6.9 1.3 %collective-permute-start.6 = (bf16[128,1024]{1,0:T(8,128)(2,1)S(1)}, bf16[128,1024]{1,0:T(8,128)(2,1)S(1)}, u32[]{:S(2)}, u32[]{:S(2)}) collective-permute-start(bf16[128,1024]{1,0:T(8,128)(2,1)S(1)} %constant_dynamic-update-slice_fusion), channel_id=1, source_target_pairs={{0,6},{1,7},{2,8},{3,9},{4,10},{5,11},{6,12},{7,13},{8,14},{9,15},... | collective-permute-start | bytes 786440 | tf_op jit(solution)/shard_map/ppermute | solution.py:254
  8.2 3.6 %collective-permute-done.refs_4_.refs_5_ = bf16[128,1024]{1,0:T(8,128)(2,1)S(1)} collective-permute-done((bf16[128,1024]{1,0:T(8,128)(2,1)S(1)}, bf16[128,1024]{1,0:T(8,128)(2,1)S(1)}, u32[]{:S(2)}, u32[]{:S(2)}) %collective-permute-start) | collective-permute-done | bytes 262176 | tf_op jit(solution)/shard_map/ppermute | solution.py:254
  11.8 3.5 %collective-permute-start.1 = (bf16[128,1024]{1,0:T(8,128)(2,1)S(1)}, bf16[128,1024]{1,0:T(8,128)(2,1)S(1)}, u32[]{:S(2)}, u32[]{:S(2)}) collective-permute-start(bf16[128,1024]{1,0:T(8,128)(2,1)S(1)} %collective-permute-done.refs_4_.refs_5_), channel_id=1, source_target_pairs={{0,2},{1,3},{2,4},{3,5},{4,6},{5,7},{6,8},{7,9},{8,10},{9,11},{10,... | collective-permute-start | bytes 786440 | tf_op jit(solution)/shard_map/ppermute | solution.py:254
  15.3 0.0 collective-permute-done.3
  15.3 1.3 %collective-permute-start.4 = (bf16[128,1024]{1,0:T(8,128)(2,1)S(1)}, bf16[128,1024]{1,0:T(8,128)(2,1)S(1)}, u32[]{:S(2)}, u32[]{:S(2)}) collective-permute-start(bf16[128,1024]{1,0:T(8,128)(2,1)S(1)} %collective-permute-done.3), channel_id=1, source_target_pairs={{0,8},{2,10},{4,12},{6,14},{8,16},{10,18},{12,20},{14,22},{16,24},... | collective-permute-start | bytes 786440 | tf_op jit(solution)/shard_map/ppermute | solution.py:254
  16.6 9.2 %collective-permute-start.8 = (bf16[128,1024]{1,0:T(8,128)(2,1)S(1)}, bf16[128,1024]{1,0:T(8,128)(2,1)S(1)}, u32[]{:S(2)}, u32[]{:S(2)}) collective-permute-start(bf16[128,1024]{1,0:T(8,128)(2,1)S(1)} %constant_dynamic-update-slice_fusion), channel_id=1, source_target_pairs={{0,8},{1,9},{2,10},{3,11},{4,12},{5,13},{6,14},{7,15},{8,16},{9,17... | collective-permute-start | bytes 786440 | tf_op jit(solution)/shard_map/ppermute | solution.py:254
  25.8 0.1 collective-permute-start.5
  25.8 0.0 collective-permute-done.6.refs_5_.refs_6_
  25.9 2.0 %collective-permute-start.7 = (bf16[128,1024]{1,0:T(8,128)(2,1)S(1)}, bf16[128,1024]{1,0:T(8,128)(2,1)S(1)}, u32[]{:S(2)}, u32[]{:S(2)}) collective-permute-start(bf16[128,1024]{1,0:T(8,128)(2,1)S(1)} %collective-permute-done.6.refs_5_.refs_6_), channel_id=1, source_target_pairs={{0,1},{1,0},{2,3},{3,2},{4,5},{5,4},{6,7},{7,6},{8,9},{9,8},{10,11... | collective-permute-start | bytes 786440 | tf_op jit(solution)/shard_map/ppermute | solution.py:254
  27.9 0.0 copy-start
  27.9 1.2 %copy-done = bf16[128,4096]{1,0:T(8,128)(2,1)S(1)} copy-done((bf16[128,4096]{1,0:T(8,128)(2,1)S(1)}, bf16[128,4096]{1,0:T(8,128)(2,1)}, u32[]{:S(2)}) %copy-start) | copy-done | bytes 1048600
  29.1 0.0 copy-start.2
  29.1 0.9 %copy-done.2 = bf16[128,512]{1,0:T(8,128)(2,1)S(1)} copy-done((bf16[128,512]{1,0:T(8,128)(2,1)S(1)}, bf16[128,512]{1,0:T(8,128)(2,1)}, u32[]{:S(2)}) %copy-start.2) | copy-done | bytes 131096
  30.0 0.0 copy-start.3
  30.0 0.9 %copy-done.3 = bf16[128,512]{1,0:T(8,128)(2,1)S(1)} copy-done((bf16[128,512]{1,0:T(8,128)(2,1)S(1)}, bf16[128,512]{1,0:T(8,128)(2,1)}, u32[]{:S(2)}) %copy-start.3) | copy-done | bytes 131096
  30.9 0.0 copy-start.4
  30.9 0.7 copy-done.4
  31.5 0.0 copy-start.1
  31.5 4.3 %shard_map.46 = (f32[128,4096]{1,0:T(8,128)S(1)}, f32[4,128,128]{2,1,0:T(8,128)S(1)}, s32[128,128]{1,0:T(8,128)S(1)}) custom-call(s32[16]{0:T(128)S(1)} %copy-done.4, bf16[128,4096]{1,0:T(8,128)(2,1)S(1)} %copy-done, bf16[128,512]{1,0:T(8,128)(2,1)S(1)} %copy-done.2, bf16[128,512]{1,0:T(8,128)(2,1)S(1)} %copy-done.3, ...), custom_call_target="tpu_custom_call" | custom-call | flops 536870912 | bytes 4194304 | tf_op jit(solution)/shard_map/pallas_call | solution.py:226
  35.8 0.0 collective-permute-done.1.refs_11_.refs_12_
  35.9 0.1 collective-permute-start.2
  36.0 0.0 collective-permute-done.4
  36.0 0.0 collective-permute-done.8.refs_9_.refs_10_
  36.0 0.0 collective-permute-done.5.refs_3_.refs_4_
  36.1 4.6 %collective-permute-done.7.refs_7_.refs_8_ = bf16[128,1024]{1,0:T(8,128)(2,1)S(1)} collective-permute-done((bf16[128,1024]{1,0:T(8,128)(2,1)S(1)}, bf16[128,1024]{1,0:T(8,128)(2,1)S(1)}, u32[]{:S(2)}, u32[]{:S(2)}) %collective-permute-start.7) | collective-permute-done | bytes 262176 | tf_op jit(solution)/shard_map/ppermute | solution.py:254
  40.6 0.0 copy-done.1
  40.6 15.1 %shard_map.47 = (f32[128,4096]{1,0:T(8,128)S(1)}, f32[4,128,128]{2,1,0:T(8,128)S(1)}) custom-call(bf16[128,4096]{1,0:T(8,128)(2,1)S(1)} %copy-done.1, bf16[128,1024]{1,0:T(8,128)(2,1)S(1)} %broadcast_select_fusion.refs_1_.refs_2_, bf16[128,1024]{1,0:T(8,128)(2,1)S(1)} %broadcast_select_fusion.refs_1_.refs_2_, ...), custom_call_target="tpu_custom_call" | custom-call | flops 1610612736 | bytes 4194304 | tf_op jit(solution)/shard_map/pallas_call | solution.py:226
  55.8 0.0 collective-permute-done.2.refs_1_.refs_2_
  55.8 12.0 %shard_map.48 = bf16[128,4096]{1,0:T(8,128)(2,1)} custom-call(bf16[128,4096]{1,0:T(8,128)(2,1)S(1)} %copy-done.1, bf16[128,1024]{1,0:T(8,128)(2,1)S(1)} %collective-permute-done.2.refs_1_.refs_2_, bf16[128,1024]{1,0:T(8,128)(2,1)S(1)} %collective-permute-done.2.refs_1_.refs_2_, f32[128,4096]{1,0:T(8,128)S(1)} %get-tuple-element.13.refs_3_, ...), custom_call_target="tpu_custom_call" | custom-call | flops 268435456 | bytes 4194304 | tf_op jit(solution)/shard_map/pallas_call | solution.py:226
  (1 shorter events, 0.0 us)
Async XLA Ops:
  1.8 9.9 %collective-permute-start = (bf16[128,1024]{1,0:T(8,128)(2,1)S(1)}, bf16[128,1024]{1,0:T(8,128)(2,1)S(1)}, u32[]{:S(2)}, u32[]{:S(2)}) collective-permute-start(bf16[128,1024]{1,0:T(8,128)(2,1)S(1)} %constant_dynamic-update-slice_fusion), channel_id=1, source_target_pairs={{0,2},{1,3},{2,4},{3,5},{4,6},{5,7},{6,8},{7,9},{8,10},{9,11},{10,... | collective-permute-start | bytes 786440 | tf_op jit(solution)/shard_map/ppermute | solution.py:254
  5.3 9.9 %collective-permute-start.3 = (bf16[128,1024]{1,0:T(8,128)(2,1)S(1)}, bf16[128,1024]{1,0:T(8,128)(2,1)S(1)}, u32[]{:S(2)}, u32[]{:S(2)}) collective-permute-start(bf16[128,1024]{1,0:T(8,128)(2,1)S(1)} %constant_dynamic-update-slice_fusion), channel_id=1, source_target_pairs={{0,1},{1,0},{2,3},{3,2},{4,5},{5,4},{6,7},{7,6},{8,9},{9,8},{10,11... | collective-permute-start | bytes 786440 | tf_op jit(solution)/shard_map/ppermute | solution.py:254
  6.9 19.0 %collective-permute-start.6 = (bf16[128,1024]{1,0:T(8,128)(2,1)S(1)}, bf16[128,1024]{1,0:T(8,128)(2,1)S(1)}, u32[]{:S(2)}, u32[]{:S(2)}) collective-permute-start(bf16[128,1024]{1,0:T(8,128)(2,1)S(1)} %constant_dynamic-update-slice_fusion), channel_id=1, source_target_pairs={{0,6},{1,7},{2,8},{3,9},{4,10},{5,11},{6,12},{7,13},{8,14},{9,15},... | collective-permute-start | bytes 786440 | tf_op jit(solution)/shard_map/ppermute | solution.py:254
  11.8 24.1 %collective-permute-start.1 = (bf16[128,1024]{1,0:T(8,128)(2,1)S(1)}, bf16[128,1024]{1,0:T(8,128)(2,1)S(1)}, u32[]{:S(2)}, u32[]{:S(2)}) collective-permute-start(bf16[128,1024]{1,0:T(8,128)(2,1)S(1)} %collective-permute-done.refs_4_.refs_5_), channel_id=1, source_target_pairs={{0,2},{1,3},{2,4},{3,5},{4,6},{5,7},{6,8},{7,9},{8,10},{9,11},{10,... | collective-permute-start | bytes 786440 | tf_op jit(solution)/shard_map/ppermute | solution.py:254
  15.3 20.7 %collective-permute-start.4 = (bf16[128,1024]{1,0:T(8,128)(2,1)S(1)}, bf16[128,1024]{1,0:T(8,128)(2,1)S(1)}, u32[]{:S(2)}, u32[]{:S(2)}) collective-permute-start(bf16[128,1024]{1,0:T(8,128)(2,1)S(1)} %collective-permute-done.3), channel_id=1, source_target_pairs={{0,8},{2,10},{4,12},{6,14},{8,16},{10,18},{12,20},{14,22},{16,24},... | collective-permute-start | bytes 786440 | tf_op jit(solution)/shard_map/ppermute | solution.py:254
  16.6 19.5 %collective-permute-start.8 = (bf16[128,1024]{1,0:T(8,128)(2,1)S(1)}, bf16[128,1024]{1,0:T(8,128)(2,1)S(1)}, u32[]{:S(2)}, u32[]{:S(2)}) collective-permute-start(bf16[128,1024]{1,0:T(8,128)(2,1)S(1)} %constant_dynamic-update-slice_fusion), channel_id=1, source_target_pairs={{0,8},{1,9},{2,10},{3,11},{4,12},{5,13},{6,14},{7,15},{8,16},{9,17... | collective-permute-start | bytes 786440 | tf_op jit(solution)/shard_map/ppermute | solution.py:254
  25.8 10.3 %collective-permute-start.5 = (bf16[128,1024]{1,0:T(8,128)(2,1)S(1)}, bf16[128,1024]{1,0:T(8,128)(2,1)S(1)}, u32[]{:S(2)}, u32[]{:S(2)}) collective-permute-start(bf16[128,1024]{1,0:T(8,128)(2,1)S(1)} %collective-permute-done.refs_4_.refs_5_), channel_id=1, source_target_pairs={{0,1},{1,0},{2,3},{3,2},{4,5},{5,4},{6,7},{7,6},{8,9},{9,8},{10,11... | collective-permute-start | bytes 786440 | tf_op jit(solution)/shard_map/ppermute | solution.py:254
  25.9 14.8 %collective-permute-start.7 = (bf16[128,1024]{1,0:T(8,128)(2,1)S(1)}, bf16[128,1024]{1,0:T(8,128)(2,1)S(1)}, u32[]{:S(2)}, u32[]{:S(2)}) collective-permute-start(bf16[128,1024]{1,0:T(8,128)(2,1)S(1)} %collective-permute-done.6.refs_5_.refs_6_), channel_id=1, source_target_pairs={{0,1},{1,0},{2,3},{3,2},{4,5},{5,4},{6,7},{7,6},{8,9},{9,8},{10,11... | collective-permute-start | bytes 786440 | tf_op jit(solution)/shard_map/ppermute | solution.py:254
  27.9 1.2 %copy-start = (bf16[128,4096]{1,0:T(8,128)(2,1)S(1)}, bf16[128,4096]{1,0:T(8,128)(2,1)}, u32[]{:S(2)}) copy-start(bf16[128,4096]{1,0:T(8,128)(2,1)} %refs_0_.5) | copy-start | bytes 3145732
  29.1 0.9 %copy-start.2 = (bf16[128,512]{1,0:T(8,128)(2,1)S(1)}, bf16[128,512]{1,0:T(8,128)(2,1)}, u32[]{:S(2)}) copy-start(bf16[128,512]{1,0:T(8,128)(2,1)} %refs_2_.1) | copy-start | bytes 393220
  30.0 0.9 %copy-start.3 = (bf16[128,512]{1,0:T(8,128)(2,1)S(1)}, bf16[128,512]{1,0:T(8,128)(2,1)}, u32[]{:S(2)}) copy-start(bf16[128,512]{1,0:T(8,128)(2,1)} %refs_3_.1) | copy-start | bytes 393220
  30.9 0.7 copy-start.4
  31.5 9.1 %copy-start.1 = (bf16[128,4096]{1,0:T(8,128)(2,1)S(1)}, bf16[128,4096]{1,0:T(8,128)(2,1)}, u32[]{:S(2)}) copy-start(bf16[128,4096]{1,0:T(8,128)(2,1)} %refs_0_.5) | copy-start | bytes 3145732
  35.9 19.9 %collective-permute-start.2 = (bf16[128,1024]{1,0:T(8,128)(2,1)S(1)}, bf16[128,1024]{1,0:T(8,128)(2,1)S(1)}, u32[]{:S(2)}, u32[]{:S(2)}) collective-permute-start(bf16[128,1024]{1,0:T(8,128)(2,1)S(1)} %collective-permute-done.1.refs_11_.refs_12_), channel_id=1, source_target_pairs={{0,1},{1,0},{2,3},{3,2},{4,5},{5,4},{6,7},{7,6},{8,9},{9,8},{10,11... | collective-permute-start | bytes 786440 | tf_op jit(solution)/shard_map/ppermute | solution.py:254
